TPU v7x, 32 devices: a whole 2x2x4 slice. The times are simulated.
32 devices in a mesh: ga: 8 (over z, y), ba: 4 (over x, core).
Axes of the slice: x: 2, y: 2, z: 4, core: 2. Of those that a mesh axis runs over, the one named last changes fastest.
Arguments:
- coefficients: bfloat16 [10240, 6144], P('ga', 'ba')
- rotation: bfloat16 [6144, 6144], P('ga', 'ba'), may hold values from -0.078125 to 0.078125
Outputs:
- new_coefficients: bfloat16 [10240, 6144], P('ga', 'ba')
- band_rms: float32 [6144], P('ba')
All inputs are finite; a program needn't handle non-finite values.
Results may differ from a plain program's by a relative error of at most 0.0004.
Values may be sent and summed in bfloat16 or wider, within the bound.
A program may use at most 128 MiB of HBM per device.

v0:
```python
import jax
import jax.numpy as jnp
from jax import lax
from jax.sharding import PartitionSpec as P


def body(coefficients, rotation):
    all_bands = lax.all_gather(coefficients, "ba", axis=1, tiled=True)
    rotated = jnp.dot(
        all_bands,
        lax.all_gather(rotation, "ga", axis=0, tiled=True),
        preferred_element_type=jnp.float32,
    )
    squares = lax.psum(jnp.sum(rotated * rotated, axis=0), "ga")
    total_rows = coefficients.shape[0] * lax.axis_size("ga")
    band_rms = jnp.sqrt(squares / total_rows + 1e-06)
    return ((rotated / band_rms).astype(jnp.bfloat16), band_rms)


def solution(mesh):
    in_specs = (P("ga", "ba"), P("ga", "ba"))
    out_specs = (P("ga", "ba"), P("ba"))
    return jax.shard_map(body, mesh=mesh, in_specs=in_specs, out_specs=out_specs, check_vma=False)
```

profile of v0, /device:TPU:0, one launch (start us, length us, event | category | flops | bytes accessed | tf_op | source)
XLA Modules:
  0.0 543.6 jit_solution(14183646409815637874)
XLA Ops:
  7.2 0.0 all-gather.3.cloned.1.call-start
  7.2 0.7 all-gather.3.cloned.1.call-update
  7.9 0.0 all-gather.5.cloned.1.call-start
  7.9 0.7 all-gather.5.cloned.1.call-update
  8.6 103.6 %all-gather.3.cloned.1.call-done = bf16[1280,6144]{1,0:T(8,128)(2,1)} async-done(((bf16[1280,1536]{1,0:T(8,128)(2,1)}), bf16[1280,6144]{1,0:T(8,128)(2,1)}) %all-gather.3.cloned.1.call-update) | async-done | bytes 15728656 | tf_op jit(solution)/shard_map/all_gather | solution.py:8
  112.2 364.0 %all-gather.5.cloned.1.call-done = bf16[6144,1536]{1,0:T(8,128)(2,1)} async-done(((bf16[768,1536]{1,0:T(8,128)(2,1)}), bf16[6144,1536]{1,0:T(8,128)(2,1)}) %all-gather.5.cloned.1.call-update) | async-done | bytes 18874384 | tf_op jit(solution)/shard_map/all_gather | solution.py:11
  476.2 33.9 %multiply_reduce_fusion = (f32[1536]{0:T(1024)S(1)}, f32[1280,1536]{1,0:T(8,128)}) fusion(bf16[1280,6144]{1,0:T(8,128)(2,1)} %all-gather.3.cloned.1.call-done, bf16[6144,1536]{1,0:T(8,128)(2,1)} %all-gather.5.cloned.1.call-done), kind=kOutput, calls=%fused_computation.1 | convolution fusion | flops 24163121152 | bytes 42473472 | tf_op jit(solution)/shard_map/dot_general | solution.py:9
  510.1 20.4 %psum.7 = f32[1536]{0:T(1024)S(1)} all-reduce(f32[1536]{0:T(1024)S(1)} %get-tuple-element.2), channel_id=1, replica_groups=mesh['ga'=8,'ba'=4] {'ga'}, use_global_device_ids=true, to_apply=%region_1.0 | all-reduce | flops 1536 | bytes 12288 | tf_op jit(solution)/shard_map/psum | solution.py:14
  530.6 0.0 copy-start
  530.6 6.2 %divide_convert_fusion = bf16[1280,1536]{1,0:T(8,128)(2,1)} fusion(f32[1280,1536]{1,0:T(8,128)} %get-tuple-element.3, f32[1536]{0:T(1024)S(1)} %add_sqrt_fusion), kind=kLoop, calls=%fused_computation | loop fusion | flops 3932160 | bytes 11802624 | tf_op jit(solution)/shard_map/convert_element_type | solution.py:17
  536.8 0.0 copy-done
  (1 shorter events, 0.0 us)
Async XLA Ops:
  7.2 105.1 %all-gather.3.cloned.1.call-start = ((), (), s32[]{:S(2)}) async-start(), calls=%async_computation | async-start | bytes 19660800 | tf_op jit(solution)/shard_map/all_gather | solution.py:8
  7.9 468.3 %all-gather.5.cloned.1.call-start = ((), (), s32[]{:S(2)}) async-start(), calls=%async_computation.1 | async-start | bytes 21233664 | tf_op jit(solution)/shard_map/all_gather | solution.py:11
  530.6 6.2 %copy-start = (f32[1536]{0:T(1024)}, f32[1536]{0:T(1024)S(1)}, u32[]{:S(2)}) copy-start(f32[1536]{0:T(1024)S(1)} %add_sqrt_fusion) | copy-start | bytes 18436
Sparse Core Ops, SparseCore 0:
  9.5 102.6 all-gather.2
  113.8 362.3 all-gather.4
where the time goes:
time: 544 us
  waiting for transfers between devices  469 us (86%)
  matrix products  33.9 us (6%)
  blocking collectives  20.4 us (4%)
  between operations  14.1 us (3%)
  other arithmetic  6.19 us (1%)
    all_gather x1, waiting for transfers between devices, body(): lax.all_gather(rotation, 'ga', axis=0, tiled=True)  364 us
    all_gather x1, waiting for transfers between devices, body(): all_bands = lax.all_gather(coefficients, 'ba', axis=1, tiled=True)  104 us
    dot_general x1, matrix products, body(): jnp.dot(all_bands, lax.all_gather(rotation, 'ga', axis=0, tiled=True), pr...  33.9 us
    psum x1, blocking collectives, body(): squares = lax.psum(jnp.sum(rotated * rotated, axis=0), 'ga')  20.4 us
  transfers between devices with their start and end apart: 2, of which 2 were waited for; matrix products, arithmetic and copies ran while one was open for 0% of the time, Pallas kernels for 0%

commit v1 on v0

--- a/solution.py
+++ b/solution.py
@@ -5,7 +5,10 @@
 
 
 def body(coefficients, rotation):
-    all_bands = lax.all_gather(coefficients, "ba", axis=1, tiled=True)
+    size = lax.axis_size("ba")
+    blocks = jnp.stack([coefficients for _ in range(size)])
+    blocks = lax.all_to_all(blocks, "ba", split_axis=0, concat_axis=0)
+    all_bands = jnp.concatenate(blocks, axis=1)
     rotated = jnp.dot(
         all_bands,
         lax.all_gather(rotation, "ga", axis=0, tiled=True),

time: 544 us -> 443 us (0.81)
  waiting for transfers between devices: 469 us -> 181 us
  blocking collectives: 20.4 us -> 197 us
  local copies, waits for them, and re-layouts: 0.01 us -> 10 us
    all_gather x1, waiting for transfers between devices: 364 us -> 180 us  [body(): lax.all_gather(rotation, 'ga', axis=0, tiled=True)]
    all_to_all x0 -> x1, blocking collectives: none -> 177 us  [body(): blocks = lax.all_to_all(blocks, 'ba', split_axis=0, concat_axis=0)]
    all_gather x1 -> x0, waiting for transfers between devices: 104 us -> none  [body(): all_bands = lax.all_gather(coefficients, 'ba', axis=1, tiled=True)]
    unnamed x2 -> x3, local copies, waits for them, and re-layouts: 0.01 us -> 6.27 us
  transfers between devices with their start and end apart: 2 -> 1, of which waited for: 2 -> 1; matrix products, arithmetic and copies ran while one was open for 0% -> 2% of each run, Pallas kernels for 0% -> 0%
where the time goes in v1:
time: 443 us; the launch traced here: 442 us
  blocking collectives  197 us (44%)
  waiting for transfers between devices  181 us (41%)
  matrix products  34 us (8%)
  between operations  14.1 us (3%)
  local copies, waits for them, and re-layouts  10 us (2%)
  other arithmetic  6.19 us (1%)
    all_gather x1, waiting for transfers between devices, body(): lax.all_gather(rotation, 'ga', axis=0, tiled=True)  180 us
    all_to_all x1, blocking collectives, body(): blocks = lax.all_to_all(blocks, 'ba', split_axis=0, concat_axis=0)  177 us
    dot_general x1, matrix products, body(): jnp.dot(all_bands, lax.all_gather(rotation, 'ga', axis=0, tiled=True), pr...  34 us
    psum x1, blocking collectives, body(): squares = lax.psum(jnp.sum(rotated * rotated, axis=0), 'ga')  20.4 us
  transfers between devices with their start and end apart: 1, of which 1 were waited for; matrix products, arithmetic and copies ran while one was open for 2% of the time, Pallas kernels for 0%

profile of v1, /device:TPU:0, one launch (start us, length us, event | category | flops | bytes accessed | tf_op | source)
XLA Modules:
  0.0 442.2 jit_solution(4590798612077796172)
XLA Ops:
  7.2 0.0 all-gather.2.cloned.1.call-start
  7.2 0.7 all-gather.2.cloned.1.call-update
  7.9 6.3 %copy.4 = bf16[1280,1536]{0,1:T(8,128)(2,1)} copy(bf16[1280,1536]{1,0:T(8,128)(2,1)} %param.2) | data formatting | bytes 7864320 | tf_op args[0]
  14.2 3.8 stack.2
  17.9 176.8 %all_to_all.5 = bf16[4,1280,1536]{1,2,0:T(8,128)(2,1)} all-to-all(bf16[4,1280,1536]{1,2,0:T(8,128)(2,1)S(1)} %stack.2), channel_id=1, replica_groups=mesh['ga'=8,'ba'=4] {'ba'}, dimensions={0} | all-to-all | bytes 31457280 | tf_op jit(solution)/shard_map/all_to_all | solution.py:10
  194.7 179.9 %all-gather.2.cloned.1.call-done = bf16[6144,1536]{1,0:T(8,128)(2,1)} async-done(((bf16[768,1536]{1,0:T(8,128)(2,1)}), bf16[6144,1536]{1,0:T(8,128)(2,1)}) %all-gather.2.cloned.1.call-update) | async-done | bytes 18874384 | tf_op jit(solution)/shard_map/all_gather | solution.py:14
  374.7 34.0 %multiply_reduce_fusion = (f32[1536]{0:T(1024)S(1)}, f32[1280,1536]{1,0:T(8,128)}) fusion(bf16[1280,6144]{0,1:T(8,128)(2,1)} %bitcast.5, bf16[6144,1536]{1,0:T(8,128)(2,1)} %all-gather.2.cloned.1.call-done), kind=kOutput, calls=%fused_computation.1 | convolution fusion | flops 24163121152 | bytes 42473472 | tf_op jit(solution)/shard_map/dot_general | solution.py:12
  408.7 20.4 %psum.7 = f32[1536]{0:T(1024)S(1)} all-reduce(f32[1536]{0:T(1024)S(1)} %get-tuple-element.2), channel_id=1, replica_groups=mesh['ga'=8,'ba'=4] {'ga'}, use_global_device_ids=true, to_apply=%region_1.0 | all-reduce | flops 1536 | bytes 12288 | tf_op jit(solution)/shard_map/psum | solution.py:17
  429.2 0.0 copy-start
  429.2 6.2 %divide_convert_fusion = bf16[1280,1536]{1,0:T(8,128)(2,1)} fusion(f32[1280,1536]{1,0:T(8,128)} %get-tuple-element.3, f32[1536]{0:T(1024)S(1)} %add_sqrt_fusion), kind=kLoop, calls=%fused_computation | loop fusion | flops 3932160 | bytes 11802624 | tf_op jit(solution)/shard_map/convert_element_type | solution.py:20
  435.3 0.0 copy-done
  (1 shorter events, 0.0 us)
Async XLA Ops:
  7.2 367.5 %all-gather.2.cloned.1.call-start = ((), (), s32[]{:S(2)}) async-start(), calls=%async_computation.1 | async-start | bytes 21233664 | tf_op jit(solution)/shard_map/all_gather | solution.py:14
  429.2 6.2 %copy-start = (f32[1536]{0:T(1024)}, f32[1536]{0:T(1024)S(1)}, u32[]{:S(2)}) copy-start(f32[1536]{0:T(1024)S(1)} %add_sqrt_fusion) | copy-start | bytes 18436
Sparse Core Ops, SparseCore 0:
  9.5 365.1 all-gather.1
